TPU v7x, 32 devices: a whole 2x2x4 slice. The times are simulated.
32 devices in a mesh: row: 8 (over z, core), col: 4 (over y, x).
Axes of the slice: x: 2, y: 2, z: 4, core: 2. Of those that a mesh axis runs over, the one named last changes fastest.
Arguments:
- pair_exchange: bfloat16 [64, 16, 1024], P(('row', 'col')), may hold values from -6 to 6
- conduction: bfloat16 [64, 4, 1024], P(('row', 'col')), may hold values from -6 to 6
- valence: bfloat16 [64, 4, 1024], P(('row', 'col')), may hold values from -6 to 6
- coulomb: float32 [1024], replicated, may hold values from 0.5 to 5
- screening: float32 [34, 1024], replicated, may hold values from 0.1 to 1
- energies: float32 [64, 16], P(('row', 'col')), may hold values from 1 to 9
- vectors: bfloat16 [64, 512], P(('row', 'col')), may hold values from -6 to 6
- k_coords: int32 [64, 2], P(('row', 'col')), may hold values from 0 to 31, as said below
Outputs:
- residual_block: float32 [64, 512], P(('row', 'col'))
- alpha: float32 [32, 32], replicated
Inputs may be any that keep to these rules, and one draw needn't show every extreme that they name: `k_coords`: each row holds a k-point's coordinates on the periodic 32 x 2 mesh, first then second; every mesh point occurs exactly once.
All inputs are finite; a program needn't handle non-finite values.
Results may differ from a plain program's by a relative error of at most 0.0028.
Values may be sent and summed in bfloat16 or wider, within the bound.
A program may use at most 64 MiB of HBM per device.

v0:
```python
import jax
import jax.numpy as jnp
from jax import lax
from jax.sharding import PartitionSpec as P

MX = 32
highest = lax.Precision.HIGHEST


def pair_factors(conduction, valence):
    count, valence_count, plane_count = valence.shape
    joined = (
        valence.astype(jnp.float32)[:, :, None, :] * conduction.astype(jnp.float32)[:, None, :, :]
    )
    return joined.reshape(count, valence_count * conduction.shape[1], plane_count).astype(
        jnp.bfloat16
    )


def transfer_index(rows_at, cols_at, mesh_cols):
    delta_first = jnp.mod(rows_at[:, None, 0] - cols_at[None, :, 0], MX)
    delta_second = jnp.mod(rows_at[:, None, 1] - cols_at[None, :, 1], mesh_cols)
    fold_first = jnp.minimum(delta_first, MX - delta_first)
    fold_second = jnp.minimum(delta_second, mesh_cols - delta_second)
    return (fold_first * (mesh_cols // 2 + 1) + fold_second).astype(jnp.int32)


def on_device(pair_exchange, conduction, valence, coulomb, screening, energies, vectors, k_coords):
    local_count, band_count, plane_count = pair_exchange.shape
    vector_count = vectors.shape[1] // band_count
    row_count = lax.axis_size("row")
    col_count = lax.axis_size("col")
    total_count = local_count * row_count * col_count
    mesh_cols = total_count // MX
    moving = vectors.reshape(local_count, band_count, vector_count)
    partial_density = jnp.einsum(
        "ktg,ktn->gn", pair_exchange, moving, preferred_element_type=jnp.float32
    )
    density = lax.psum(partial_density, ("row", "col"))
    block_size = 128
    sweeps = plane_count // block_size
    col_cond, col_val, col_vec, col_at = (
        lax.all_gather(conduction, "row", axis=0, tiled=True),
        lax.all_gather(valence, "row", axis=0, tiled=True),
        lax.all_gather(vectors, "row", axis=0, tiled=True),
        lax.all_gather(k_coords, "row", axis=0, tiled=True),
    )
    row_cond, row_val, row_at = (
        lax.all_gather(conduction, "col", axis=0, tiled=True),
        lax.all_gather(valence, "col", axis=0, tiled=True),
        lax.all_gather(k_coords, "col", axis=0, tiled=True),
    )
    row_pairs = pair_factors(row_cond, row_val)
    col_pairs = pair_factors(col_cond, col_val)
    indices = transfer_index(row_at, col_at, mesh_cols)
    col_moving = col_vec.reshape(-1, band_count, vector_count)

    def square_sweep(sweep_index, running):
        anchor = sweep_index * block_size
        coupling = jnp.take(
            lax.dynamic_slice_in_dim(screening, anchor, block_size, 1), indices, axis=0
        )
        row_block = lax.dynamic_slice_in_dim(row_pairs, anchor, block_size, 2)
        col_block = lax.dynamic_slice_in_dim(col_pairs, anchor, block_size, 2)
        col_proj = jnp.einsum(
            "ktg,ktn->kng", col_block, col_moving, preferred_element_type=jnp.float32
        )
        potential = jnp.einsum("ijg,jng->ing", coupling, col_proj, precision=highest)
        return running + jnp.einsum(
            "ktg,kng->ktn", row_block.astype(jnp.float32), potential, precision=highest
        )

    forward = lax.fori_loop(
        0,
        sweeps,
        square_sweep,
        jnp.zeros((row_pairs.shape[0], band_count, vector_count), jnp.float32),
    )
    owned = lax.psum_scatter(
        forward.reshape(col_count, local_count, band_count, vector_count),
        "col",
        scatter_dimension=0,
        tiled=True,
    )[0]
    moving_wide = moving.astype(jnp.float32)
    exchange_term = jnp.einsum(
        "ktg,gn->ktn", pair_exchange.astype(jnp.float32) * coulomb, density, precision=highest
    )
    applied = (
        energies[:, :, None] * moving_wide
        + 2.0 / (total_count * band_count) * exchange_term
        - owned / total_count
    )
    gram = jnp.einsum("ktm,ktn->mn", moving_wide, applied, precision=highest)
    alpha = lax.psum(gram, ("row", "col")) / (total_count * band_count)
    residual = applied - jnp.einsum("ktm,mn->ktn", moving_wide, alpha, precision=highest)
    return (residual.reshape(local_count, band_count * vector_count), alpha)


def solution(mesh):
    in_specs = (
        P(("row", "col"), None, None),
        P(("row", "col"), None, None),
        P(("row", "col"), None, None),
        P(),
        P(),
        P(("row", "col"), None),
        P(("row", "col"), None),
        P(("row", "col"), None),
    )
    out_specs = (P(("row", "col"), None), P())
    return jax.shard_map(
        on_device, mesh=mesh, in_specs=in_specs, out_specs=out_specs, check_vma=False
    )
```

profile of v0, /device:TPU:0, one launch (start us, length us, event | category | flops | bytes accessed | tf_op | source)
XLA Modules:
  0.0 299.9 jit_solution(13418184121838847277)
XLA Ops:
  8.7 13.5 %all-gather.2 = s32[8,2,2]{2,1,0:T(2,128)S(1)} all-gather(s32[1,2,2]{2,1,0:T(2,128)S(1)} %bitcast.65), channel_id=1, replica_groups=mesh['row'=8,'col'=4] {'row'}, dimensions={0}, use_global_device_ids=true | all-gather | bytes 144 | tf_op jit(solution)/shard_map/all_gather | solution.py:46
  22.1 8.1 %all-gather.1 = s32[4,2,2]{2,1,0:T(2,128)S(1)} all-gather(s32[1,2,2]{2,1,0:T(2,128)S(1)} %bitcast.66), channel_id=1, replica_groups=mesh['row'=8,'col'=4] {'col'}, dimensions={0}, use_global_device_ids=true | all-gather | bytes 80 | tf_op jit(solution)/shard_map/all_gather | solution.py:51
  30.2 14.3 %all_gather.23 = bf16[16,4,1024]{2,1,0:T(4,128)(2,1)S(1)} all-gather(bf16[2,4,1024]{2,1,0:T(4,128)(2,1)} %param.12), channel_id=1, replica_groups=mesh['row'=8,'col'=4] {'row'}, dimensions={0}, use_global_device_ids=true | all-gather | bytes 147456 | tf_op jit(solution)/shard_map/all_gather | solution.py:44
  44.5 8.3 %all_gather.21 = bf16[8,4,1024]{2,1,0:T(4,128)(2,1)S(1)} all-gather(bf16[2,4,1024]{2,1,0:T(4,128)(2,1)S(1)} %copy-done.2), channel_id=1, replica_groups=mesh['row'=8,'col'=4] {'col'}, dimensions={0}, use_global_device_ids=true | all-gather | bytes 81920 | tf_op jit(solution)/shard_map/all_gather | solution.py:50
  52.9 14.0 %all_gather.24 = bf16[16,4,1024]{2,1,0:T(4,128)(2,1)S(1)} all-gather(bf16[2,4,1024]{2,1,0:T(4,128)(2,1)S(1)} %copy-done.3), channel_id=1, replica_groups=mesh['row'=8,'col'=4] {'row'}, dimensions={0}, use_global_device_ids=true | all-gather | bytes 147456 | tf_op jit(solution)/shard_map/all_gather | solution.py:43
  66.9 7.2 %all_gather.22 = bf16[8,4,1024]{2,1,0:T(4,128)(2,1)S(1)} all-gather(bf16[2,4,1024]{2,1,0:T(4,128)(2,1)S(1)} %copy-done.3), channel_id=1, replica_groups=mesh['row'=8,'col'=4] {'col'}, dimensions={0}, use_global_device_ids=true | all-gather | bytes 81920 | tf_op jit(solution)/shard_map/all_gather | solution.py:49
  75.8 12.8 %all-gather = bf16[8,2,512]{2,1,0:T(2,128)(2,1)S(1)} all-gather(bf16[1,2,512]{2,1,0:T(2,128)(2,1)S(1)} %bitcast.64), channel_id=1, replica_groups=mesh['row'=8,'col'=4] {'row'}, dimensions={0}, use_global_device_ids=true | all-gather | bytes 18432 | tf_op jit(solution)/shard_map/all_gather | solution.py:45
  88.7 33.2 %while.14 = (s32[]{:T(128)}, f32[8,16,32]{2,1,0:T(8,128)S(1)}, bf16[8,16,1024]{2,1,0:T(8,128)(2,1)S(1)}, bf16[16,16,1024]{2,1,0:T(8,128)(2,1)S(1)}, bf16[16,16,3...) while((s32[]{:T(128)}, f32[8,16,32]{2,1,0:T(8,128)S(1)}, ...), condition=%wide.region_2.3_spmd.clone, body=%wide.region_1.2_spmd.clone.sunk | while | flops 14714503 | bytes 2319689 | solution.py:73
  88.7 0.7 constant_dynamic-slice_fusion.2
  89.6 0.6 gather_fusion
  91.4 1.1 convolution_bitcast_fusion.8
  92.9 0.7 constant_dynamic-slice_fusion.2
  95.5 1.1 convolution_bitcast_fusion.8
  97.0 0.7 constant_dynamic-slice_fusion.2
  99.7 1.1 convolution_bitcast_fusion.8
  101.2 0.7 constant_dynamic-slice_fusion.2
  103.8 1.1 convolution_bitcast_fusion.8
  105.3 0.7 constant_dynamic-slice_fusion.2
  108.0 1.1 convolution_bitcast_fusion.8
  109.5 0.7 constant_dynamic-slice_fusion.2
  112.1 1.1 convolution_bitcast_fusion.8
  113.6 0.7 constant_dynamic-slice_fusion.2
  116.3 1.1 convolution_bitcast_fusion.8
  117.8 0.7 constant_dynamic-slice_fusion.2
  120.4 1.1 convolution_bitcast_fusion.8
  122.8 0.9 convolution_bitcast_fusion.2
  123.7 20.8 %reduce-scatter.4.cloned.1.call-done = f32[1,2,16,32]{3,2,1,0:T(8,128)} async-done(((f32[4,2,16,32]{3,2,1,0:T(8,128)}), f32[1,2,16,32]{3,2,1,0:T(8,128)}) %reduce-scatter.4.cloned.1.call-update) | async-done | bytes 4112
  144.5 105.8 %all-reduce.3.cloned.1.call-done = f32[1024,32]{0,1:T(8,128)} async-done(((f32[1024,32]{0,1:T(8,128)}), f32[1024,32]{0,1:T(8,128)}) %all-reduce.3.cloned.1.call-update) | async-done | bytes 131088 | tf_op jit(solution)/shard_map/psum | solution.py:39
  250.3 1.1 fusion.17
  251.7 39.3 %psum.15 = f32[32,32]{0,1:T(8,128)S(1)} all-reduce(f32[32,32]{0,1:T(8,128)S(1)} %convolution_bitcast_fusion.4), channel_id=1, replica_groups=mesh['row'=8,'col'=4] {'row','col'}, use_global_device_ids=true, to_apply=%region_4.5 | all-reduce | flops 1024 | bytes 8192 | tf_op jit(solution)/shard_map/psum | solution.py:95
  291.1 0.7 reshape.61
  291.8 0.7 copy.24
  (111 shorter events, 21.2 us)
Async XLA Ops:
  8.0 0.7 copy-start.6
  8.0 136.5 %reduce-scatter.4.cloned.1.call-start = ((), (), s32[]{:S(2)}) async-start(), calls=%async_computation.2 | async-start | bytes 81920
  30.2 14.3 %copy-start.2 = (bf16[2,4,1024]{2,1,0:T(4,128)(2,1)S(1)}, bf16[2,4,1024]{2,1,0:T(4,128)(2,1)}, u32[]{:S(2)}) copy-start(bf16[2,4,1024]{2,1,0:T(4,128)(2,1)} %param.12) | copy-start | bytes 49156
  44.5 8.3 %copy-start.3 = (bf16[2,4,1024]{2,1,0:T(4,128)(2,1)S(1)}, bf16[2,4,1024]{2,1,0:T(4,128)(2,1)}, u32[]{:S(2)}) copy-start(bf16[2,4,1024]{2,1,0:T(4,128)(2,1)} %param.11) | copy-start | bytes 49156
  75.2 0.7 copy-start.4
  121.9 0.6 copy-start
  121.9 0.9 copy-start.1
  122.6 127.7 %all-reduce.3.cloned.1.call-start = ((), (), s32[]{:S(2)}) async-start(), calls=%async_computation.1 | async-start | bytes 262144 | tf_op jit(solution)/shard_map/psum | solution.py:39
  123.7 126.6 %copy-start.5 = (f32[1024]{0:T(1024)S(1)}, f32[1024]{0:T(1024)}, u32[]{:S(2)}) copy-start(f32[1024]{0:T(1024)} %param.13) | copy-start | bytes 12292
  123.7 126.7 %copy-start.7 = (f32[2,16]{1,0:T(2,128)S(1)}, f32[2,16]{1,0:T(2,128)}, u32[]{:S(2)}) copy-start(f32[2,16]{1,0:T(2,128)} %param.15) | copy-start | bytes 388
Sparse Core Ops, SparseCore 0:
  122.7 21.7 reduce-scatter.3
Sparse Core Ops, SparseCore 1:
  128.6 121.7 all-reduce.2
where the time goes:
time: 301 us; the launch traced here: 300 us
  waiting for transfers between devices  127 us (42%)
  blocking collectives  117 us (39%)
  local copies, waits for them, and re-layouts  21.7 us (7%)
  matrix products  16.1 us (5%)
  between operations  15.6 us (5%)
    psum x1, waiting for transfers between devices, on_device(): density = lax.psum(partial_density, ('row', 'col'))  106 us
    psum x1, blocking collectives, on_device(): alpha = lax.psum(gram, ('row', 'col')) / (total_count * band_count)  39.3 us
    unnamed x3, waiting for transfers between devices  20.8 us
    all_gather x1, blocking collectives, on_device(): lax.all_gather(valence, 'row', axis=0, tiled=True)  14.3 us
    all_gather x1, blocking collectives, on_device(): lax.all_gather(conduction, 'row', axis=0, tiled=True)  14 us
    all_gather x1, blocking collectives, on_device(): lax.all_gather(k_coords, 'row', axis=0, tiled=True)  13.5 us
    all_gather x1, blocking collectives, on_device(): lax.all_gather(vectors, 'row', axis=0, tiled=True)  12.8 us
    dot_general x8, matrix products, square_sweep(): jnp.einsum('ijg,jng->ing', coupling, col_proj, precision=highest)  8.7 us
  transfers between devices with their start and end apart: 2, of which 2 were waited for; matrix products, arithmetic and copies ran while one was open for 0% of the time, Pallas kernels for 0%

commit v1 on v0

--- a/solution.py
+++ b/solution.py
@@ -36,7 +36,7 @@
     partial_density = jnp.einsum(
         "ktg,ktn->gn", pair_exchange, moving, preferred_element_type=jnp.float32
     )
-    density = lax.psum(partial_density, ("row", "col"))
+    density = jnp.sum(lax.all_gather(partial_density, ("row", "col")), axis=0)
     block_size = 128
     sweeps = plane_count // block_size
     col_cond, col_val, col_vec, col_at = (

time: 301 us -> 197 us (0.65)
  waiting for transfers between devices: 127 us -> 16.6 us
  local copies, waits for them, and re-layouts: 21.7 us -> 25.7 us
    psum x1 -> x0, waiting for transfers between devices: 106 us -> none  [on_device(): density = lax.psum(partial_density, ('row', 'col'))]
    unnamed x3, waiting for transfers between devices: 20.8 us -> 16.5 us
    unnamed x21 -> x16, local copies, waits for them, and re-layouts: 2.95 us -> 6.24 us
  transfers between devices with their start and end apart: 2 -> 2, of which waited for: 2 -> 1; matrix products, arithmetic and copies ran while one was open for 0% -> 20% of each run, Pallas kernels for 0% -> 0%
where the time goes in v1:
time: 197 us; the launch traced here: 196 us
  blocking collectives  119 us (60%)
  local copies, waits for them, and re-layouts  25.7 us (13%)
  matrix products  16.7 us (8%)
  waiting for transfers between devices  16.6 us (8%)
  between operations  15.6 us (8%)
  other arithmetic  2.48 us (1%)
    psum x1, blocking collectives, on_device(): alpha = lax.psum(gram, ('row', 'col')) / (total_count * band_count)  39.3 us
    unnamed x3, waiting for transfers between devices  16.5 us
    all_gather x1, blocking collectives, on_device(): lax.all_gather(conduction, 'row', axis=0, tiled=True)  14.5 us
    all_gather x1, blocking collectives, on_device(): lax.all_gather(valence, 'row', axis=0, tiled=True)  14.2 us
    all_gather x1, blocking collectives, on_device(): lax.all_gather(vectors, 'row', axis=0, tiled=True)  12.8 us
    all_gather x1, blocking collectives, on_device(): lax.all_gather(k_coords, 'row', axis=0, tiled=True)  12 us
    all_gather x1, blocking collectives, on_device(): lax.all_gather(conduction, 'col', axis=0, tiled=True)  9.89 us
    dot_general x8, matrix products, square_sweep(): jnp.einsum('ijg,jng->ing', coupling, col_proj, precision=highest)  8.73 us
  transfers between devices with their start and end apart: 2, of which 1 were waited for; matrix products, arithmetic and copies ran while one was open for 20% of the time, Pallas kernels for 0%

profile of v1, /device:TPU:0, one launch (start us, length us, event | category | flops | bytes accessed | tf_op | source)
XLA Modules:
  0.0 196.3 jit_solution(12537116921025192922)
XLA Ops:
  8.1 0.8 reshape.58
  8.8 1.7 convolution_bitcast_fusion.2
  10.6 9.9 %all_gather.30 = bf16[8,4,1024]{2,1,0:T(4,128)(2,1)S(1)} all-gather(bf16[2,4,1024]{2,1,0:T(4,128)(2,1)} %param.11), channel_id=1, replica_groups=mesh['row'=8,'col'=4] {'col'}, dimensions={0}, use_global_device_ids=true | all-gather | bytes 81920 | tf_op jit(solution)/shard_map/all_gather | solution.py:49
  20.5 14.5 %all_gather.32 = bf16[16,4,1024]{2,1,0:T(4,128)(2,1)S(1)} all-gather(bf16[2,4,1024]{2,1,0:T(4,128)(2,1)} %param.11), channel_id=1, replica_groups=mesh['row'=8,'col'=4] {'row'}, dimensions={0}, use_global_device_ids=true | all-gather | bytes 147456 | tf_op jit(solution)/shard_map/all_gather | solution.py:43
  35.0 8.2 %all_gather.29 = bf16[8,4,1024]{2,1,0:T(4,128)(2,1)S(1)} all-gather(bf16[2,4,1024]{2,1,0:T(4,128)(2,1)} %param.12), channel_id=1, replica_groups=mesh['row'=8,'col'=4] {'col'}, dimensions={0}, use_global_device_ids=true | all-gather | bytes 81920 | tf_op jit(solution)/shard_map/all_gather | solution.py:50
  43.3 14.2 %all_gather.31 = bf16[16,4,1024]{2,1,0:T(4,128)(2,1)S(1)} all-gather(bf16[2,4,1024]{2,1,0:T(4,128)(2,1)} %param.12), channel_id=1, replica_groups=mesh['row'=8,'col'=4] {'row'}, dimensions={0}, use_global_device_ids=true | all-gather | bytes 147456 | tf_op jit(solution)/shard_map/all_gather | solution.py:44
  57.5 12.0 %all-gather.3 = s32[8,2,2]{2,1,0:T(2,128)S(1)} all-gather(s32[1,2,2]{2,1,0:T(2,128)} %bitcast.71), channel_id=1, replica_groups=mesh['row'=8,'col'=4] {'row'}, dimensions={0}, use_global_device_ids=true | all-gather | bytes 144 | tf_op jit(solution)/shard_map/all_gather | solution.py:46
  69.6 7.6 %all-gather.2 = s32[4,2,2]{2,1,0:T(2,128)S(1)} all-gather(s32[1,2,2]{2,1,0:T(2,128)} %bitcast.72), channel_id=1, replica_groups=mesh['row'=8,'col'=4] {'col'}, dimensions={0}, use_global_device_ids=true | all-gather | bytes 80 | tf_op jit(solution)/shard_map/all_gather | solution.py:51
  77.8 12.8 %all-gather.1 = bf16[8,2,512]{2,1,0:T(2,128)(2,1)S(1)} all-gather(bf16[1,2,512]{2,1,0:T(2,128)(2,1)S(1)} %bitcast.70), channel_id=1, replica_groups=mesh['row'=8,'col'=4] {'row'}, dimensions={0}, use_global_device_ids=true | all-gather | bytes 18432 | tf_op jit(solution)/shard_map/all_gather | solution.py:45
  91.2 33.2 %while.14 = (s32[]{:T(128)}, f32[8,16,32]{2,1,0:T(8,128)S(1)}, bf16[8,16,1024]{2,1,0:T(8,128)(2,1)S(1)}, bf16[16,16,1024]{2,1,0:T(8,128)(2,1)S(1)}, bf16[16,16,3...) while((s32[]{:T(128)}, f32[8,16,32]{2,1,0:T(8,128)S(1)}, ...), condition=%wide.region_2.3_spmd.clone, body=%wide.region_1.2_spmd.clone.sunk | while | flops 14714503 | bytes 2319697 | solution.py:73
  91.9 0.7 constant_dynamic-slice_fusion.2
  93.8 1.1 convolution_bitcast_fusion.8
  96.1 0.7 constant_dynamic-slice_fusion.2
  98.0 1.1 convolution_bitcast_fusion.8
  100.2 0.7 constant_dynamic-slice_fusion.2
  102.1 1.1 convolution_bitcast_fusion.8
  104.4 0.7 constant_dynamic-slice_fusion.2
  106.3 1.1 convolution_bitcast_fusion.8
  108.6 0.7 constant_dynamic-slice_fusion.2
  110.5 1.1 convolution_bitcast_fusion.8
  112.7 0.7 constant_dynamic-slice_fusion.2
  114.6 1.1 convolution_bitcast_fusion.8
  116.9 0.7 constant_dynamic-slice_fusion.2
  118.8 1.1 convolution_bitcast_fusion.8
  121.0 0.7 constant_dynamic-slice_fusion.2
  122.9 1.1 convolution_bitcast_fusion.8
  125.1 4.6 %copy.33 = f32[4,8,32,1024]{3,2,1,0:T(8,128)S(1)} copy(f32[4,8,32,1024]{3,1,2,0:T(8,128)} %bitcast.62) | data formatting | bytes 8388608
  130.4 16.5 %reduce-scatter.4.cloned.1.call-done = f32[1,2,16,32]{3,2,1,0:T(8,128)} async-done(((f32[4,2,16,32]{3,2,1,0:T(8,128)}), f32[1,2,16,32]{3,2,1,0:T(8,128)}) %reduce-scatter.4.cloned.1.call-update) | async-done | bytes 4112
  146.9 1.0 fusion.17
  148.0 39.3 %psum.7 = f32[32,32]{0,1:T(8,128)S(1)} all-reduce(f32[32,32]{0,1:T(8,128)S(1)} %convolution_bitcast_fusion.4), channel_id=1, replica_groups=mesh['row'=8,'col'=4] {'row','col'}, use_global_device_ids=true, to_apply=%region_4.5 | all-reduce | flops 1024 | bytes 8192 | tf_op jit(solution)/shard_map/psum | solution.py:95
  187.5 0.7 reshape.61
  188.2 0.7 copy.24
  (107 shorter events, 21.1 us)
Async XLA Ops:
  8.0 69.8 %copy-start.2 = (bf16[2,512]{1,0:T(2,128)(2,1)S(1)}, bf16[2,512]{1,0:T(2,128)(2,1)}, u32[]{:S(2)}) copy-start(bf16[2,512]{1,0:T(2,128)(2,1)} %param.16) | copy-start | bytes 6148
  8.0 117.1 %all-gather.6.cloned.1.call-start = ((), (), s32[]{:S(2)}) async-start(), calls=%async_computation.1 | async-start | bytes 4325376 | tf_op jit(solution)/shard_map/all_gather | solution.py:39
  10.5 136.3 %reduce-scatter.4.cloned.1.call-start = ((), (), s32[]{:S(2)}) async-start(), calls=%async_computation.2 | async-start | bytes 81920
  124.4 0.6 copy-start
  129.7 17.2 %copy-start.1 = (bf16[2,16,1024]{2,1,0:T(8,128)(2,1)S(1)}, bf16[2,16,1024]{2,1,0:T(8,128)(2,1)}, u32[]{:S(2)}) copy-start(bf16[2,16,1024]{2,1,0:T(8,128)(2,1)} %param.10) | copy-start | bytes 196612
  129.7 17.2 %copy-start.3 = (f32[1024]{0:T(1024)S(1)}, f32[1024]{0:T(1024)}, u32[]{:S(2)}) copy-start(f32[1024]{0:T(1024)} %param.13) | copy-start | bytes 12292
  129.7 17.1 %copy-start.4 = (f32[2,16]{1,0:T(2,128)S(1)}, f32[2,16]{1,0:T(2,128)}, u32[]{:S(2)}) copy-start(f32[2,16]{1,0:T(2,128)} %param.15) | copy-start | bytes 388
Sparse Core Ops, SparseCore 0:
  11.7 65.3 all-gather.5
Sparse Core Ops, SparseCore 1:
  125.2 21.7 reduce-scatter.3
